TPU v7x, 32 devices: a whole 2x2x4 slice. The times are simulated.
32 devices in a mesh: gx: 2 (over y), gy: 4 (over x, core), gz: 4 (over z).
Axes of the slice: x: 2, y: 2, z: 4, core: 2. Of those that a mesh axis runs over, the one named last changes fastest.
Arguments:
- loads: float32 [16, 4, 16, 1024], P(None, 'gx', 'gy', 'gz'), may hold values from -60 to 60
- moduli: float32 [8], replicated, may hold values from 0.5 to 4
- material: int32 [4, 16, 1024], P('gx', 'gy', 'gz'), may hold values from 0 to 7
Outputs:
- solution: float32 [16, 4, 16, 1024], P(None, 'gx', 'gy', 'gz')
- residual: float32 [16, 4, 16, 1024], P(None, 'gx', 'gy', 'gz')
All inputs are finite; a program needn't handle non-finite values.
Results may differ from a plain program's by a relative error of at most 0.005.
The roundings to bfloat16 on the way count: a program that leaves them out, or rounds other values in their place, can miss the bound.
Values may be sent and summed in bfloat16 or wider, within the bound.
A program may use at most 64 MiB of HBM per device.

v0:
```python
import jax
import jax.numpy as jnp
import numpy as np
from jax import lax
from jax.sharding import PartitionSpec as P

ITERS = 2
SIGMA = 0.25


def padded_2(cells, sides, width):
    for axis, dim in sides:
        count = lax.axis_size(axis)
        ends = count - 1
        head = lax.slice_in_dim(cells, 0, width, axis=dim)
        tail = lax.slice_in_dim(cells, cells.shape[dim] - width, cells.shape[dim], axis=dim)
        cells = jnp.concatenate(
            [
                lax.ppermute(tail, axis, [(i, (i + 1) % count) for i in range(ends)]),
                cells,
                lax.ppermute(head, axis, [((i + 1) % count, i) for i in range(ends)]),
            ],
            axis=dim,
        )
    return cells


def stiffness_table():
    line_mass = np.array([[1.0 / 3.0, 1.0 / 6.0], [1.0 / 6.0, 1.0 / 3.0]])
    line_stiff = np.array([[1.0, -1.0], [-1.0, 1.0]])
    table = np.zeros((8, 8))
    for target in range(8):
        for source in range(8):
            target_bits = [target >> 2 & 1, target >> 1 & 1, target & 1]
            source_bits = [source >> 2 & 1, source >> 1 & 1, source & 1]
            total = 0.0
            for stiff_dim in range(3):
                factor = 1.0
                for other in range(3):
                    if other == stiff_dim:
                        factor = factor * line_stiff[target_bits[other], source_bits[other]]
                    else:
                        factor = factor * line_mass[target_bits[other], source_bits[other]]
                total = total + factor
            table[target, source] = total
    return table


def corner_bits(corner):
    return (corner >> 2 & 1, corner >> 1 & 1, corner & 1)


def apply_operator(field, weights, kernel):
    lowered = field.astype(jnp.bfloat16)
    padded = padded_2(lowered, (("gx", 1), ("gy", 2), ("gz", 3)), 1)
    size_x, size_y, size_z = (field.shape[1], field.shape[2], field.shape[3])
    pieces = []
    for corner in range(8):
        bit_x, bit_y, bit_z = corner_bits(corner)
        pieces.append(
            padded[
                :,
                bit_x : bit_x + size_x + 1,
                bit_y : bit_y + size_y + 1,
                bit_z : bit_z + size_z + 1,
            ]
        )
    stacked = jnp.stack(pieces)
    total = SIGMA * field
    for corner in range(8):
        bit_x, bit_y, bit_z = corner_bits(corner)
        part = (
            jnp.einsum("b,bcxyz->cxyz", kernel[corner], stacked, preferred_element_type=jnp.float32)
            * weights
        )
        total = (
            total
            + part[
                :,
                1 - bit_x : 1 - bit_x + size_x,
                1 - bit_y : 1 - bit_y + size_y,
                1 - bit_z : 1 - bit_z + size_z,
            ]
        )
    return total


def local_gram(left, right):
    return jnp.einsum("cxyz,dxyz->cd", left, right, precision=lax.Precision.HIGHEST)


def combine(block, coeffs):
    return jnp.einsum("cxyz,cd->dxyz", block, coeffs, precision=lax.Precision.HIGHEST)


def solve_small(matrix, rhs_small):
    factor = jnp.linalg.cholesky(matrix)
    return jax.scipy.linalg.cho_solve((factor, True), rhs_small)


def residual_gram(residual):
    return lax.psum(local_gram(residual, residual), ("gx", "gy", "gz"))


def on_device(loads, moduli, material):
    kernel = jnp.asarray(stiffness_table(), jnp.float32).astype(jnp.bfloat16)
    levels = jnp.arange(moduli.shape[0], dtype=jnp.int32)
    node_modulus = jnp.sum(jnp.where(material[..., None] == levels, moduli, 0.0), axis=-1)
    padded_mod = padded_2(node_modulus, (("gx", 0), ("gy", 1), ("gz", 2)), 1)
    size_x, size_y, size_z = material.shape
    weights = jnp.zeros((size_x + 1, size_y + 1, size_z + 1), jnp.float32)
    for corner in range(8):
        bit_x, bit_y, bit_z = corner_bits(corner)
        weights = (
            weights
            + padded_mod[
                bit_x : bit_x + size_x + 1, bit_y : bit_y + size_y + 1, bit_z : bit_z + size_z + 1
            ]
        )
    weights = weights * 0.125
    solution = jnp.zeros_like(loads)
    residual = loads
    direction = loads
    current = residual_gram(residual)
    for iteration in range(ITERS):
        image = apply_operator(direction, weights, kernel)
        curvature, cross, image_sq = lax.psum(
            (local_gram(direction, image), local_gram(image, residual), local_gram(image, image)),
            ("gx", "gy", "gz"),
        )
        alpha = solve_small(curvature, current)
        solution = solution + combine(direction, alpha)
        residual = residual - combine(image, alpha)
        if iteration + 1 < ITERS:
            high = lax.Precision.HIGHEST
            cross_term = jnp.dot(alpha.T, cross, precision=high)
            quad_term = jnp.dot(jnp.dot(alpha.T, image_sq, precision=high), alpha, precision=high)
            updated = current - cross_term - cross_term.T + quad_term
            beta = solve_small(current, updated)
            direction = residual + combine(direction, beta)
            current = updated
    return (solution, residual)


def solution(mesh):
    in_specs = (P(None, "gx", "gy", "gz"), P(), P("gx", "gy", "gz"))
    out_specs = (P(None, "gx", "gy", "gz"), P(None, "gx", "gy", "gz"))
    return jax.shard_map(
        on_device, mesh=mesh, in_specs=in_specs, out_specs=out_specs, check_vma=False
    )
```

profile of v0, /device:TPU:0, one launch (start us, length us, event | category | flops | bytes accessed | tf_op | source)
XLA Modules:
  0.0 185.7 jit_solution(12359744168205889732)
XLA Ops:
  1.4 4.9 %collective-permute-start.6 = (f32[1,4,256]{2,1,0:T(4,128)S(1)}, f32[1,4,256]{2,1,0:T(4,128)S(1)}, u32[]{:S(2)}, u32[]{:S(2)}) collective-permute-start(f32[1,4,256]{2,1,0:T(4,128)S(1)} %get-tuple-element.42), channel_id=1, source_target_pairs={{0,16},{1,17},{2,18},{3,19},{4,20},{5,21},{6,22},{7,23},{8,24},{9,... | collective-permute-start | bytes 12296 | tf_op jit(solution)/shard_map/ppermute | solution.py:19
  6.4 1.3 collective-permute-start.7
  8.6 4.5 %collective-permute-start = (bf16[16,1,4,256]{3,2,1,0:T(4,128)(2,1)S(1)}, bf16[16,1,4,256]{3,2,1,0:T(4,128)(2,1)S(1)}, u32[]{:S(2)}, u32[]{:S(2)}) collective-permute-start(bf16[16,1,4,256]{3,2,1,0:T(4,128)(2,1)S(1)} %get-tuple-element.26), channel_id=1, source_target_pairs={{0,16},{1,17},{2,18},{3,19},{4,20},{5,21},{6,22},{7,23},{8,24},{9,... | collective-permute-start | bytes 98312 | tf_op jit(solution)/shard_map/ppermute | solution.py:19
  13.2 1.3 collective-permute-start.1
  14.5 1.3 collective-permute-start.8
  15.8 1.3 collective-permute-start.9
  17.1 1.3 convolution_bitcast_fusion.4
  18.4 2.2 %collective-permute-done.9 = f32[4,1,256]{2,1,0:T(1,128)S(1)} collective-permute-done((f32[4,1,256]{2,1,0:T(1,128)S(1)}, f32[4,1,256]{2,1,0:T(1,128)S(1)}, u32[]{:S(2)}, u32[]{:S(2)}) %collective-permute-start.9) | collective-permute-done | bytes 4128 | tf_op jit(solution)/shard_map/ppermute | solution.py:21
  20.7 3.5 %collective-permute-start.10 = (f32[4,6,1]{2,1,0:T(8,128)S(1)}, f32[4,6,1]{2,1,0:T(8,128)S(1)}, u32[]{:S(2)}, u32[]{:S(2)}) collective-permute-start(f32[4,6,1]{2,1,0:T(8,128)S(1)} %get-tuple-element.36), channel_id=1, source_target_pairs={{0,1},{1,2},{2,3},{4,5},{5,6},{6,7},{8,9},{9,10},{10,11},{12,13},{... | collective-permute-start | bytes 296 | tf_op jit(solution)/shard_map/ppermute | solution.py:19
  24.2 1.3 collective-permute-start.11
  25.6 4.2 %collective-permute-done.11 = f32[4,6,1]{2,1,0:T(8,128)S(1)} collective-permute-done((f32[4,6,1]{2,1,0:T(8,128)S(1)}, f32[4,6,1]{2,1,0:T(8,128)S(1)}, u32[]{:S(2)}, u32[]{:S(2)}) %collective-permute-start.11) | collective-permute-done | bytes 128 | tf_op jit(solution)/shard_map/ppermute | solution.py:21
  30.1 2.8 %collective-permute-start.2 = (bf16[16,4,1,256]{3,2,1,0:T(2,128)(2,1)S(1)}, bf16[16,4,1,256]{3,2,1,0:T(2,128)(2,1)S(1)}, u32[]{:S(2)}, u32[]{:S(2)}) collective-permute-start(bf16[16,4,1,256]{3,2,1,0:T(2,128)(2,1)S(1)} %get-tuple-element.22), channel_id=1, source_target_pairs={{0,4},{4,8},{8,12},{1,5},{5,9},{9,13},{2,6},{6,10},{10,14},{3,7},{... | collective-permute-start | bytes 98312 | tf_op jit(solution)/shard_map/ppermute | solution.py:19
  33.0 1.3 collective-permute-start.3
  34.3 2.8 %collective-permute-done.3 = bf16[16,4,1,256]{3,2,1,0:T(2,128)(2,1)S(1)} collective-permute-done((bf16[16,4,1,256]{3,2,1,0:T(2,128)(2,1)S(1)}, bf16[16,4,1,256]{3,2,1,0:T(2,128)(2,1)S(1)}, u32[]{:S(2)}, u32[]{:S(2)}) %collective-permute-start.3) | collective-permute-done | bytes 32800 | tf_op jit(solution)/shard_map/ppermute | solution.py:21
  37.5 3.5 %collective-permute-start.4 = (bf16[16,4,6,1]{3,2,1,0:T(8,128)(2,1)S(1)}, bf16[16,4,6,1]{3,2,1,0:T(8,128)(2,1)S(1)}, u32[]{:S(2)}, u32[]{:S(2)}) collective-permute-start(bf16[16,4,6,1]{3,2,1,0:T(8,128)(2,1)S(1)} %get-tuple-element.15), channel_id=1, source_target_pairs={{0,1},{1,2},{2,3},{4,5},{5,6},{6,7},{8,9},{9,10},{10,11},{12,13},{... | collective-permute-start | bytes 2312 | tf_op jit(solution)/shard_map/ppermute | solution.py:19
  41.0 1.3 collective-permute-start.5
  43.5 4.4 %collective-permute-done.5 = bf16[16,4,6,1]{3,2,1,0:T(8,128)(2,1)S(1)} collective-permute-done((bf16[16,4,6,1]{3,2,1,0:T(8,128)(2,1)S(1)}, bf16[16,4,6,1]{3,2,1,0:T(8,128)(2,1)S(1)}, u32[]{:S(2)}, u32[]{:S(2)}) %collective-permute-start.5) | collective-permute-done | bytes 800 | tf_op jit(solution)/shard_map/ppermute | solution.py:21
  49.3 1.6 copy.46
  57.3 43.2 %all-reduce = (f32[16,16]{0,1:T(8,128)S(1)}, f32[16,16]{0,1:T(8,128)S(1)}, f32[16,16]{1,0:T(8,128)S(1)}, f32[16,16]{1,0:T(8,128)S(1)}) all-reduce(f32[16,16]{0,1:T(8,128)S(1)} %convolution_bitcast_fusion.4, f32[16,16]{0,1:T(8,128)S(1)} %bitcast.265, ...), channel_id=1, replica_groups=mesh['gx'=2,'gy'=4,'gz'=4] {'gx','gy','gz'}, use_global_device_ids=true, to_apply=%region_4.0 | all-reduce | flops 1024 | bytes 8192 | tf_op jit(solution)/shard_map/psum | solution.py:102
  100.6 1.5 cholesky.70
  104.7 1.5 cholesky.59
  110.8 4.2 %collective-permute-start.12 = (bf16[16,1,4,256]{3,0,2,1:T(8,128)(2,1)S(1)}, bf16[16,1,4,256]{3,0,2,1:T(8,128)(2,1)S(1)}, u32[]{:S(2)}, u32[]{:S(2)}) collective-permute-start(bf16[16,1,4,256]{3,0,2,1:T(8,128)(2,1)S(1)} %get-tuple-element.24), channel_id=1, source_target_pairs={{0,16},{1,17},{2,18},{3,19},{4,20},{5,21},{6,22},{7,23},{8,24},{9,... | collective-permute-start | bytes 98312 | tf_op jit(solution)/shard_map/ppermute | solution.py:19
  115.0 1.3 collective-permute-start.13
  116.6 4.2 %collective-permute-done.13 = bf16[16,1,4,256]{3,0,2,1:T(8,128)(2,1)S(1)} collective-permute-done((bf16[16,1,4,256]{3,0,2,1:T(8,128)(2,1)S(1)}, bf16[16,1,4,256]{3,0,2,1:T(8,128)(2,1)S(1)}, u32[]{:S(2)}, u32[]{:S(2)}) %collective-permute-start.13) | collective-permute-done | bytes 32800 | tf_op jit(solution)/shard_map/ppermute | solution.py:21
  120.8 1.3 collective-permute-start.14
  122.1 1.3 collective-permute-start.15
  123.5 2.1 %collective-permute-done.15 = bf16[16,4,1,256]{3,0,2,1:T(8,128)(2,1)S(1)} collective-permute-done((bf16[16,4,1,256]{3,0,2,1:T(8,128)(2,1)S(1)}, bf16[16,4,1,256]{3,0,2,1:T(8,128)(2,1)S(1)}, u32[]{:S(2)}, u32[]{:S(2)}) %collective-permute-start.15) | collective-permute-done | bytes 32800 | tf_op jit(solution)/shard_map/ppermute | solution.py:21
  125.7 2.3 %collective-permute-start.16 = (bf16[16,4,6,1]{3,0,2,1:T(8,128)(2,1)S(1)}, bf16[16,4,6,1]{3,0,2,1:T(8,128)(2,1)S(1)}, u32[]{:S(2)}, u32[]{:S(2)}) collective-permute-start(bf16[16,4,6,1]{3,0,2,1:T(8,128)(2,1)S(1)} %get-tuple-element.19), channel_id=1, source_target_pairs={{0,1},{1,2},{2,3},{4,5},{5,6},{6,7},{8,9},{9,10},{10,11},{12,13},{... | collective-permute-start | bytes 2312 | tf_op jit(solution)/shard_map/ppermute | solution.py:19
  128.1 1.3 collective-permute-start.17
  130.3 4.3 %collective-permute-done.17 = bf16[16,4,6,1]{3,0,2,1:T(8,128)(2,1)S(1)} collective-permute-done((bf16[16,4,6,1]{3,0,2,1:T(8,128)(2,1)S(1)}, bf16[16,4,6,1]{3,0,2,1:T(8,128)(2,1)S(1)}, u32[]{:S(2)}, u32[]{:S(2)}) %collective-permute-start.17) | collective-permute-done | bytes 800 | tf_op jit(solution)/shard_map/ppermute | solution.py:21
  140.0 39.1 %psum.39 = f32[16,16]{0,1:T(8,128)S(1)} all-reduce(f32[16,16]{0,1:T(8,128)S(1)} %convolution_bitcast_fusion.1), channel_id=1, replica_groups=mesh['gx'=2,'gy'=4,'gz'=4] {'gx','gy','gz'}, use_global_device_ids=true, to_apply=%region_7.10 | all-reduce | flops 256 | bytes 2048 | tf_op jit(solution)/shard_map/psum | solution.py:127
  179.3 1.5 cholesky.81
  (133 shorter events, 30.4 us)
Async XLA Ops:
  1.4 13.0 %collective-permute-start.6 = (f32[1,4,256]{2,1,0:T(4,128)S(1)}, f32[1,4,256]{2,1,0:T(4,128)S(1)}, u32[]{:S(2)}, u32[]{:S(2)}) collective-permute-start(f32[1,4,256]{2,1,0:T(4,128)S(1)} %get-tuple-element.42), channel_id=1, source_target_pairs={{0,16},{1,17},{2,18},{3,19},{4,20},{5,21},{6,22},{7,23},{8,24},{9,... | collective-permute-start | bytes 12296 | tf_op jit(solution)/shard_map/ppermute | solution.py:19
  6.4 8.1 %collective-permute-start.7 = (f32[1,4,256]{2,1,0:T(4,128)S(1)}, f32[1,4,256]{2,1,0:T(4,128)S(1)}, u32[]{:S(2)}, u32[]{:S(2)}) collective-permute-start(f32[1,4,256]{2,1,0:T(4,128)S(1)} %get-tuple-element.43), channel_id=1, source_target_pairs={{16,0},{17,1},{18,2},{19,3},{20,4},{21,5},{22,6},{23,7},{24,8},{25... | collective-permute-start | bytes 12296 | tf_op jit(solution)/shard_map/ppermute | solution.py:21
  8.6 21.3 %collective-permute-start = (bf16[16,1,4,256]{3,2,1,0:T(4,128)(2,1)S(1)}, bf16[16,1,4,256]{3,2,1,0:T(4,128)(2,1)S(1)}, u32[]{:S(2)}, u32[]{:S(2)}) collective-permute-start(bf16[16,1,4,256]{3,2,1,0:T(4,128)(2,1)S(1)} %get-tuple-element.26), channel_id=1, source_target_pairs={{0,16},{1,17},{2,18},{3,19},{4,20},{5,21},{6,22},{7,23},{8,24},{9,... | collective-permute-start | bytes 98312 | tf_op jit(solution)/shard_map/ppermute | solution.py:19
  13.2 16.8 %collective-permute-start.1 = (bf16[16,1,4,256]{3,2,1,0:T(4,128)(2,1)S(1)}, bf16[16,1,4,256]{3,2,1,0:T(4,128)(2,1)S(1)}, u32[]{:S(2)}, u32[]{:S(2)}) collective-permute-start(bf16[16,1,4,256]{3,2,1,0:T(4,128)(2,1)S(1)} %get-tuple-element.27), channel_id=1, source_target_pairs={{16,0},{17,1},{18,2},{19,3},{20,4},{21,5},{22,6},{23,7},{24,8},{25... | collective-permute-start | bytes 98312 | tf_op jit(solution)/shard_map/ppermute | solution.py:21
  14.5 3.9 %collective-permute-start.8 = (f32[4,1,256]{2,1,0:T(1,128)S(1)}, f32[4,1,256]{2,1,0:T(1,128)S(1)}, u32[]{:S(2)}, u32[]{:S(2)}) collective-permute-start(f32[4,1,256]{2,1,0:T(1,128)S(1)} %get-tuple-element.40), channel_id=1, source_target_pairs={{0,4},{4,8},{8,12},{1,5},{5,9},{9,13},{2,6},{6,10},{10,14},{3,7},{... | collective-permute-start | bytes 12296 | tf_op jit(solution)/shard_map/ppermute | solution.py:19
  15.8 4.8 %collective-permute-start.9 = (f32[4,1,256]{2,1,0:T(1,128)S(1)}, f32[4,1,256]{2,1,0:T(1,128)S(1)}, u32[]{:S(2)}, u32[]{:S(2)}) collective-permute-start(f32[4,1,256]{2,1,0:T(1,128)S(1)} %get-tuple-element.41), channel_id=1, source_target_pairs={{4,0},{8,4},{12,8},{5,1},{9,5},{13,9},{6,2},{10,6},{14,10},{7,3},{... | collective-permute-start | bytes 12296 | tf_op jit(solution)/shard_map/ppermute | solution.py:21
  20.7 4.9 %collective-permute-start.10 = (f32[4,6,1]{2,1,0:T(8,128)S(1)}, f32[4,6,1]{2,1,0:T(8,128)S(1)}, u32[]{:S(2)}, u32[]{:S(2)}) collective-permute-start(f32[4,6,1]{2,1,0:T(8,128)S(1)} %get-tuple-element.36), channel_id=1, source_target_pairs={{0,1},{1,2},{2,3},{4,5},{5,6},{6,7},{8,9},{9,10},{10,11},{12,13},{... | collective-permute-start | bytes 296 | tf_op jit(solution)/shard_map/ppermute | solution.py:19
  24.2 5.6 %collective-permute-start.11 = (f32[4,6,1]{2,1,0:T(8,128)S(1)}, f32[4,6,1]{2,1,0:T(8,128)S(1)}, u32[]{:S(2)}, u32[]{:S(2)}) collective-permute-start(f32[4,6,1]{2,1,0:T(8,128)S(1)} %get-tuple-element.37), channel_id=1, source_target_pairs={{1,0},{2,1},{3,2},{5,4},{6,5},{7,6},{9,8},{10,9},{11,10},{13,12},{... | collective-permute-start | bytes 296 | tf_op jit(solution)/shard_map/ppermute | solution.py:21
  30.1 4.2 %collective-permute-start.2 = (bf16[16,4,1,256]{3,2,1,0:T(2,128)(2,1)S(1)}, bf16[16,4,1,256]{3,2,1,0:T(2,128)(2,1)S(1)}, u32[]{:S(2)}, u32[]{:S(2)}) collective-permute-start(bf16[16,4,1,256]{3,2,1,0:T(2,128)(2,1)S(1)} %get-tuple-element.22), channel_id=1, source_target_pairs={{0,4},{4,8},{8,12},{1,5},{5,9},{9,13},{2,6},{6,10},{10,14},{3,7},{... | collective-permute-start | bytes 98312 | tf_op jit(solution)/shard_map/ppermute | solution.py:19
  33.0 4.2 %collective-permute-start.3 = (bf16[16,4,1,256]{3,2,1,0:T(2,128)(2,1)S(1)}, bf16[16,4,1,256]{3,2,1,0:T(2,128)(2,1)S(1)}, u32[]{:S(2)}, u32[]{:S(2)}) collective-permute-start(bf16[16,4,1,256]{3,2,1,0:T(2,128)(2,1)S(1)} %get-tuple-element.23), channel_id=1, source_target_pairs={{4,0},{8,4},{12,8},{5,1},{9,5},{13,9},{6,2},{10,6},{14,10},{7,3},{... | collective-permute-start | bytes 98312 | tf_op jit(solution)/shard_map/ppermute | solution.py:21
  37.5 6.0 %collective-permute-start.4 = (bf16[16,4,6,1]{3,2,1,0:T(8,128)(2,1)S(1)}, bf16[16,4,6,1]{3,2,1,0:T(8,128)(2,1)S(1)}, u32[]{:S(2)}, u32[]{:S(2)}) collective-permute-start(bf16[16,4,6,1]{3,2,1,0:T(8,128)(2,1)S(1)} %get-tuple-element.15), channel_id=1, source_target_pairs={{0,1},{1,2},{2,3},{4,5},{5,6},{6,7},{8,9},{9,10},{10,11},{12,13},{... | collective-permute-start | bytes 2312 | tf_op jit(solution)/shard_map/ppermute | solution.py:19
  41.0 6.9 %collective-permute-start.5 = (bf16[16,4,6,1]{3,2,1,0:T(8,128)(2,1)S(1)}, bf16[16,4,6,1]{3,2,1,0:T(8,128)(2,1)S(1)}, u32[]{:S(2)}, u32[]{:S(2)}) collective-permute-start(bf16[16,4,6,1]{3,2,1,0:T(8,128)(2,1)S(1)} %get-tuple-element.14), channel_id=1, source_target_pairs={{1,0},{2,1},{3,2},{5,4},{6,5},{7,6},{9,8},{10,9},{11,10},{13,12},{... | collective-permute-start | bytes 2312 | tf_op jit(solution)/shard_map/ppermute | solution.py:21
  49.3 1.6 copy-start.1
  51.0 0.7 copy-start.2
  51.0 1.2 copy-start.3
  51.6 1.1 copy-start.4
  52.2 1.1 copy-start.5
  52.7 1.1 copy-start.6
  53.3 1.1 copy-start.7
  53.8 1.1 copy-start.8
  55.6 0.9 copy-start
  110.8 5.8 %collective-permute-start.12 = (bf16[16,1,4,256]{3,0,2,1:T(8,128)(2,1)S(1)}, bf16[16,1,4,256]{3,0,2,1:T(8,128)(2,1)S(1)}, u32[]{:S(2)}, u32[]{:S(2)}) collective-permute-start(bf16[16,1,4,256]{3,0,2,1:T(8,128)(2,1)S(1)} %get-tuple-element.24), channel_id=1, source_target_pairs={{0,16},{1,17},{2,18},{3,19},{4,20},{5,21},{6,22},{7,23},{8,24},{9,... | collective-permute-start | bytes 98312 | tf_op jit(solution)/shard_map/ppermute | solution.py:19
  115.0 5.8 %collective-permute-start.13 = (bf16[16,1,4,256]{3,0,2,1:T(8,128)(2,1)S(1)}, bf16[16,1,4,256]{3,0,2,1:T(8,128)(2,1)S(1)}, u32[]{:S(2)}, u32[]{:S(2)}) collective-permute-start(bf16[16,1,4,256]{3,0,2,1:T(8,128)(2,1)S(1)} %get-tuple-element.25), channel_id=1, source_target_pairs={{16,0},{17,1},{18,2},{19,3},{20,4},{21,5},{22,6},{23,7},{24,8},{25... | collective-permute-start | bytes 98312 | tf_op jit(solution)/shard_map/ppermute | solution.py:21
  120.8 2.6 %collective-permute-start.14 = (bf16[16,4,1,256]{3,0,2,1:T(8,128)(2,1)S(1)}, bf16[16,4,1,256]{3,0,2,1:T(8,128)(2,1)S(1)}, u32[]{:S(2)}, u32[]{:S(2)}) collective-permute-start(bf16[16,4,1,256]{3,0,2,1:T(8,128)(2,1)S(1)} %get-tuple-element.20), channel_id=1, source_target_pairs={{0,4},{4,8},{8,12},{1,5},{5,9},{9,13},{2,6},{6,10},{10,14},{3,7},{... | collective-permute-start | bytes 98312 | tf_op jit(solution)/shard_map/ppermute | solution.py:19
  122.1 3.5 %collective-permute-start.15 = (bf16[16,4,1,256]{3,0,2,1:T(8,128)(2,1)S(1)}, bf16[16,4,1,256]{3,0,2,1:T(8,128)(2,1)S(1)}, u32[]{:S(2)}, u32[]{:S(2)}) collective-permute-start(bf16[16,4,1,256]{3,0,2,1:T(8,128)(2,1)S(1)} %get-tuple-element.21), channel_id=1, source_target_pairs={{4,0},{8,4},{12,8},{5,1},{9,5},{13,9},{6,2},{10,6},{14,10},{7,3},{... | collective-permute-start | bytes 98312 | tf_op jit(solution)/shard_map/ppermute | solution.py:21
  125.7 4.5 %collective-permute-start.16 = (bf16[16,4,6,1]{3,0,2,1:T(8,128)(2,1)S(1)}, bf16[16,4,6,1]{3,0,2,1:T(8,128)(2,1)S(1)}, u32[]{:S(2)}, u32[]{:S(2)}) collective-permute-start(bf16[16,4,6,1]{3,0,2,1:T(8,128)(2,1)S(1)} %get-tuple-element.19), channel_id=1, source_target_pairs={{0,1},{1,2},{2,3},{4,5},{5,6},{6,7},{8,9},{9,10},{10,11},{12,13},{... | collective-permute-start | bytes 2312 | tf_op jit(solution)/shard_map/ppermute | solution.py:19
  128.1 6.5 %collective-permute-start.17 = (bf16[16,4,6,1]{3,0,2,1:T(8,128)(2,1)S(1)}, bf16[16,4,6,1]{3,0,2,1:T(8,128)(2,1)S(1)}, u32[]{:S(2)}, u32[]{:S(2)}) collective-permute-start(bf16[16,4,6,1]{3,0,2,1:T(8,128)(2,1)S(1)} %get-tuple-element.18), channel_id=1, source_target_pairs={{1,0},{2,1},{3,2},{5,4},{6,5},{7,6},{9,8},{10,9},{11,10},{13,12},{... | collective-permute-start | bytes 2312 | tf_op jit(solution)/shard_map/ppermute | solution.py:21
where the time goes:
time: 187 us; the launch traced here: 186 us
  blocking collectives  82.4 us (44%)
  starting transfers between devices  40 us (21%)
  waiting for transfers between devices  26.4 us (14%)
  other arithmetic  15.8 us (8%)
  matrix products  13.6 us (7%)
  local copies, waits for them, and re-layouts  6.08 us (3%)
    psum x1, blocking collectives, residual_gram(): return lax.psum(local_gram(residual, residual), ('gx', 'gy', 'gz'))  43.2 us
    psum x1, blocking collectives, on_device(): lax.psum((local_gram(direction, image), local_gram(image, residual), loca...  39.1 us
    ppermute x9, starting transfers between devices, padded_2(): lax.ppermute(tail, axis, [(i, (i + 1) % count) for i in range(ends)])  28.4 us
    ppermute x9, waiting for transfers between devices, padded_2(): lax.ppermute(head, axis, [((i + 1) % count, i) for i in range(ends)])  24.2 us
    ppermute x9, starting transfers between devices, padded_2(): lax.ppermute(head, axis, [((i + 1) % count, i) for i in range(ends)])  11.6 us
    dot_general x16, matrix products, apply_operator(): jnp.einsum('b,bcxyz->cxyz', kernel[corner], stacked, preferred_element_ty...  8.36 us
    another operation x9, other arithmetic, solve_small(): factor = jnp.linalg.cholesky(matrix)  6.4 us
    another operation x6, other arithmetic, solve_small(): return jax.scipy.linalg.cho_solve((factor, True), rhs_small)  5.63 us
  transfers between devices with their start and end apart: 18, of which 12 were waited for; matrix products, arithmetic and copies ran while one was open for 2% of the time, Pallas kernels for 0%

commit v1 on v0

--- a/solution.py
+++ b/solution.py
@@ -3,6 +3,7 @@
 import numpy as np
 from jax import lax
 from jax.sharding import PartitionSpec as P
+from jax.lax import psum
 
 ITERS = 2
 SIGMA = 0.25
@@ -124,9 +125,9 @@
     current = residual_gram(residual)
     for iteration in range(ITERS):
         image = apply_operator(direction, weights, kernel)
-        curvature, cross, image_sq = lax.psum(
-            (local_gram(direction, image), local_gram(image, residual), local_gram(image, image)),
-            ("gx", "gy", "gz"),
+        _serve_pipes = lambda sample: psum(psum(sample, ("gy", "gz")), "gx")
+        curvature, cross, image_sq = _serve_pipes(
+            (local_gram(direction, image), local_gram(image, residual), local_gram(image, image))
         )
         alpha = solve_small(curvature, current)
         solution = solution + combine(direction, alpha)

time: 187 us -> 249 us (1.33)
  blocking collectives: 82.4 us -> 143 us
  waiting for transfers between devices: 26.4 us -> 29.9 us
    psum x1 -> x4, blocking collectives: 39.1 us -> 101 us  [on_device(): _serve_pipes = lambda sample: psum(psum(sample, ('gy', 'gz')), 'gx')]
    ppermute x9, waiting for transfers between devices: 24.2 us -> 27.8 us  [padded_2(): lax.ppermute(head, axis, [((i + 1) % count, i) for i in range(ends)])]
  transfers between devices with their start and end apart: 18 -> 18, of which waited for: 12 -> 11; matrix products, arithmetic and copies ran while one was open for 2% -> 3% of each run, Pallas kernels for 0% -> 0%
where the time goes in v1:
time: 249 us; the launch traced here: 248 us
  blocking collectives  143 us (57%)
  starting transfers between devices  38.5 us (15%)
  waiting for transfers between devices  29.9 us (12%)
  other arithmetic  15.8 us (6%)
  matrix products  13.6 us (5%)
  local copies, waits for them, and re-layouts  6.08 us (2%)
    psum x4, blocking collectives, on_device(): _serve_pipes = lambda sample: psum(psum(sample, ('gy', 'gz')), 'gx')  101 us
    psum x1, blocking collectives, residual_gram(): return lax.psum(local_gram(residual, residual), ('gx', 'gy', 'gz'))  41.7 us
    ppermute x9, waiting for transfers between devices, padded_2(): lax.ppermute(head, axis, [((i + 1) % count, i) for i in range(ends)])  27.8 us
    ppermute x9, starting transfers between devices, padded_2(): lax.ppermute(tail, axis, [(i, (i + 1) % count) for i in range(ends)])  26.9 us
    ppermute x9, starting transfers between devices, padded_2(): lax.ppermute(head, axis, [((i + 1) % count, i) for i in range(ends)])  11.6 us
    dot_general x16, matrix products, apply_operator(): jnp.einsum('b,bcxyz->cxyz', kernel[corner], stacked, preferred_element_ty...  8.39 us
    another operation x9, other arithmetic, solve_small(): factor = jnp.linalg.cholesky(matrix)  6.39 us
    another operation x6, other arithmetic, solve_small(): return jax.scipy.linalg.cho_solve((factor, True), rhs_small)  5.63 us
  transfers between devices with their start and end apart: 18, of which 11 were waited for; matrix products, arithmetic and copies ran while one was open for 3% of the time, Pallas kernels for 0%

profile of v1, /device:TPU:0, one launch (start us, length us, event | category | flops | bytes accessed | tf_op | source)
XLA Modules:
  0.0 248.4 jit_solution(16700612459024689904)
XLA Ops:
  1.6 4.9 %collective-permute-start = (bf16[16,1,4,256]{3,2,1,0:T(4,128)(2,1)S(1)}, bf16[16,1,4,256]{3,2,1,0:T(4,128)(2,1)S(1)}, u32[]{:S(2)}, u32[]{:S(2)}) collective-permute-start(bf16[16,1,4,256]{3,2,1,0:T(4,128)(2,1)S(1)} %get-tuple-element.28), channel_id=1, source_target_pairs={{0,16},{1,17},{2,18},{3,19},{4,20},{5,21},{6,22},{7,23},{8,24},{9,... | collective-permute-start | bytes 98312 | tf_op jit(solution)/shard_map/ppermute | solution.py:20
  6.5 1.3 collective-permute-start.1
  8.6 4.5 %collective-permute-start.6 = (f32[1,4,256]{2,1,0:T(4,128)S(1)}, f32[1,4,256]{2,1,0:T(4,128)S(1)}, u32[]{:S(2)}, u32[]{:S(2)}) collective-permute-start(f32[1,4,256]{2,1,0:T(4,128)S(1)} %get-tuple-element.44), channel_id=1, source_target_pairs={{0,16},{1,17},{2,18},{3,19},{4,20},{5,21},{6,22},{7,23},{8,24},{9,... | collective-permute-start | bytes 12296 | tf_op jit(solution)/shard_map/ppermute | solution.py:20
  13.2 1.3 collective-permute-start.7
  15.7 41.7 %psum.65 = f32[16,16]{0,1:T(8,128)S(1)} all-reduce(f32[16,16]{0,1:T(8,128)S(1)} %convolution_bitcast_fusion.4), channel_id=1, replica_groups=mesh['gx'=2,'gy'=4,'gz'=4] {'gx','gy','gz'}, use_global_device_ids=true, to_apply=%region_5.0 | all-reduce | flops 256 | bytes 2048 | tf_op jit(solution)/shard_map/psum | solution.py:103
  57.5 1.5 cholesky.70
  60.9 1.3 collective-permute-start.9
  64.1 2.4 collective-permute-done.9
  66.6 3.4 %collective-permute-start.10 = (f32[4,6,1]{2,1,0:T(8,128)S(1)}, f32[4,6,1]{2,1,0:T(8,128)S(1)}, u32[]{:S(2)}, u32[]{:S(2)}) collective-permute-start(f32[4,6,1]{2,1,0:T(8,128)S(1)} %get-tuple-element.38), channel_id=1, source_target_pairs={{0,1},{1,2},{2,3},{4,5},{5,6},{6,7},{8,9},{9,10},{10,11},{12,13},{... | collective-permute-start | bytes 296 | tf_op jit(solution)/shard_map/ppermute | solution.py:20
  70.0 1.3 collective-permute-start.11
  71.4 4.2 %collective-permute-done.11 = f32[4,6,1]{2,1,0:T(8,128)S(1)} collective-permute-done((f32[4,6,1]{2,1,0:T(8,128)S(1)}, f32[4,6,1]{2,1,0:T(8,128)S(1)}, u32[]{:S(2)}, u32[]{:S(2)}) %collective-permute-start.11) | collective-permute-done | bytes 128 | tf_op jit(solution)/shard_map/ppermute | solution.py:22
  76.0 2.8 %collective-permute-start.2 = (bf16[16,4,1,256]{3,2,1,0:T(2,128)(2,1)S(1)}, bf16[16,4,1,256]{3,2,1,0:T(2,128)(2,1)S(1)}, u32[]{:S(2)}, u32[]{:S(2)}) collective-permute-start(bf16[16,4,1,256]{3,2,1,0:T(2,128)(2,1)S(1)} %get-tuple-element.24), channel_id=1, source_target_pairs={{0,4},{4,8},{8,12},{1,5},{5,9},{9,13},{2,6},{6,10},{10,14},{3,7},{... | collective-permute-start | bytes 98312 | tf_op jit(solution)/shard_map/ppermute | solution.py:20
  78.8 1.3 collective-permute-start.3
  80.2 3.4 %collective-permute-done.3 = bf16[16,4,1,256]{3,2,1,0:T(2,128)(2,1)S(1)} collective-permute-done((bf16[16,4,1,256]{3,2,1,0:T(2,128)(2,1)S(1)}, bf16[16,4,1,256]{3,2,1,0:T(2,128)(2,1)S(1)}, u32[]{:S(2)}, u32[]{:S(2)}) %collective-permute-start.3) | collective-permute-done | bytes 32800 | tf_op jit(solution)/shard_map/ppermute | solution.py:22
  83.9 3.3 %collective-permute-start.4 = (bf16[16,4,6,1]{3,2,1,0:T(8,128)(2,1)S(1)}, bf16[16,4,6,1]{3,2,1,0:T(8,128)(2,1)S(1)}, u32[]{:S(2)}, u32[]{:S(2)}) collective-permute-start(bf16[16,4,6,1]{3,2,1,0:T(8,128)(2,1)S(1)} %get-tuple-element.17), channel_id=1, source_target_pairs={{0,1},{1,2},{2,3},{4,5},{5,6},{6,7},{8,9},{9,10},{10,11},{12,13},{... | collective-permute-start | bytes 2312 | tf_op jit(solution)/shard_map/ppermute | solution.py:20
  87.2 1.3 collective-permute-start.5
  89.7 4.4 %collective-permute-done.5 = bf16[16,4,6,1]{3,2,1,0:T(8,128)(2,1)S(1)} collective-permute-done((bf16[16,4,6,1]{3,2,1,0:T(8,128)(2,1)S(1)}, bf16[16,4,6,1]{3,2,1,0:T(8,128)(2,1)S(1)}, u32[]{:S(2)}, u32[]{:S(2)}) %collective-permute-start.5) | collective-permute-done | bytes 800 | tf_op jit(solution)/shard_map/ppermute | solution.py:22
  95.5 1.6 copy.46
  103.5 58.3 %all-reduce = (f32[16,16]{0,1:T(8,128)S(1)}, f32[16,16]{1,0:T(8,128)S(1)}, f32[16,16]{1,0:T(8,128)S(1)}) all-reduce(f32[16,16]{0,1:T(8,128)S(1)} %bitcast.265, f32[16,16]{1,0:T(8,128)S(1)} %convolution_bitcast_fusion.3, f32[16,16]{1,0:T(8,128)S(1)} %bitcast.266), channel_id=1, replica_groups=mesh['gx'=2,'gy'=4,'gz'=4] {'gy','gz'}, use_global_device_ids=true, to_apply=%region_1.2 | all-reduce | flops 768 | bytes 6144 | tf_op jit(solution)/shard_map/psum | solution.py:128
  161.8 7.5 %all-reduce.1 = (f32[16,16]{0,1:T(8,128)S(1)}, f32[16,16]{1,0:T(8,128)S(1)}, f32[16,16]{1,0:T(8,128)S(1)}) all-reduce(f32[16,16]{0,1:T(8,128)S(1)} %get-tuple-element.8, f32[16,16]{1,0:T(8,128)S(1)} %get-tuple-element.9, f32[16,16]{1,0:T(8,128)S(1)} %get-tuple-element.10), channel_id=1, replica_groups=mesh['gx'=2,'gy'=4,'gz'=4] {'gx'}, use_global_device_ids=true, to_apply=%region_2.3 | all-reduce | flops 768 | bytes 6144 | tf_op jit(solution)/shard_map/psum | solution.py:128
  169.4 1.5 cholesky.59
  175.5 3.4 %collective-permute-start.12 = (bf16[16,1,4,256]{3,0,2,1:T(8,128)(2,1)S(1)}, bf16[16,1,4,256]{3,0,2,1:T(8,128)(2,1)S(1)}, u32[]{:S(2)}, u32[]{:S(2)}) collective-permute-start(bf16[16,1,4,256]{3,0,2,1:T(8,128)(2,1)S(1)} %get-tuple-element.26), channel_id=1, source_target_pairs={{0,16},{1,17},{2,18},{3,19},{4,20},{5,21},{6,22},{7,23},{8,24},{9,... | collective-permute-start | bytes 98312 | tf_op jit(solution)/shard_map/ppermute | solution.py:20
  178.9 1.3 collective-permute-start.13
  180.5 4.2 %collective-permute-done.13 = bf16[16,1,4,256]{3,0,2,1:T(8,128)(2,1)S(1)} collective-permute-done((bf16[16,1,4,256]{3,0,2,1:T(8,128)(2,1)S(1)}, bf16[16,1,4,256]{3,0,2,1:T(8,128)(2,1)S(1)}, u32[]{:S(2)}, u32[]{:S(2)}) %collective-permute-start.13) | collective-permute-done | bytes 32800 | tf_op jit(solution)/shard_map/ppermute | solution.py:22
  186.0 1.3 collective-permute-start.15
  187.3 4.9 %collective-permute-done.15 = bf16[16,4,1,256]{3,0,2,1:T(8,128)(2,1)S(1)} collective-permute-done((bf16[16,4,1,256]{3,0,2,1:T(8,128)(2,1)S(1)}, bf16[16,4,1,256]{3,0,2,1:T(8,128)(2,1)S(1)}, u32[]{:S(2)}, u32[]{:S(2)}) %collective-permute-start.15) | collective-permute-done | bytes 32800 | tf_op jit(solution)/shard_map/ppermute | solution.py:22
  192.3 1.9 collective-permute-start.16
  194.2 1.3 collective-permute-start.17
  196.4 4.3 %collective-permute-done.17 = bf16[16,4,6,1]{3,0,2,1:T(8,128)(2,1)S(1)} collective-permute-done((bf16[16,4,6,1]{3,0,2,1:T(8,128)(2,1)S(1)}, bf16[16,4,6,1]{3,0,2,1:T(8,128)(2,1)S(1)}, u32[]{:S(2)}, u32[]{:S(2)}) %collective-permute-start.17) | collective-permute-done | bytes 800 | tf_op jit(solution)/shard_map/ppermute | solution.py:22
  206.2 30.6 %psum.70 = f32[16,16]{0,1:T(8,128)S(1)} all-reduce(f32[16,16]{0,1:T(8,128)S(1)} %convolution_bitcast_fusion.1), channel_id=1, replica_groups=mesh['gx'=2,'gy'=4,'gz'=4] {'gy','gz'}, use_global_device_ids=true, to_apply=%region_10.13 | all-reduce | flops 256 | bytes 2048 | tf_op jit(solution)/shard_map/psum | solution.py:128
  236.9 5.0 %psum.71 = f32[16,16]{0,1:T(8,128)S(1)} all-reduce(f32[16,16]{0,1:T(8,128)S(1)} %psum.70), channel_id=1, replica_groups=mesh['gx'=2,'gy'=4,'gz'=4] {'gx'}, use_global_device_ids=true, to_apply=%region_11.14 | all-reduce | flops 256 | bytes 2048 | tf_op jit(solution)/shard_map/psum | solution.py:128
  242.0 1.5 cholesky.81
  (136 shorter events, 34.2 us)
Async XLA Ops:
  1.6 74.2 %collective-permute-start = (bf16[16,1,4,256]{3,2,1,0:T(4,128)(2,1)S(1)}, bf16[16,1,4,256]{3,2,1,0:T(4,128)(2,1)S(1)}, u32[]{:S(2)}, u32[]{:S(2)}) collective-permute-start(bf16[16,1,4,256]{3,2,1,0:T(4,128)(2,1)S(1)} %get-tuple-element.28), channel_id=1, source_target_pairs={{0,16},{1,17},{2,18},{3,19},{4,20},{5,21},{6,22},{7,23},{8,24},{9,... | collective-permute-start | bytes 98312 | tf_op jit(solution)/shard_map/ppermute | solution.py:20
  6.5 69.3 %collective-permute-start.1 = (bf16[16,1,4,256]{3,2,1,0:T(4,128)(2,1)S(1)}, bf16[16,1,4,256]{3,2,1,0:T(4,128)(2,1)S(1)}, u32[]{:S(2)}, u32[]{:S(2)}) collective-permute-start(bf16[16,1,4,256]{3,2,1,0:T(4,128)(2,1)S(1)} %get-tuple-element.29), channel_id=1, source_target_pairs={{16,0},{17,1},{18,2},{19,3},{20,4},{21,5},{22,6},{23,7},{24,8},{25... | collective-permute-start | bytes 98312 | tf_op jit(solution)/shard_map/ppermute | solution.py:22
  8.6 51.0 %collective-permute-start.6 = (f32[1,4,256]{2,1,0:T(4,128)S(1)}, f32[1,4,256]{2,1,0:T(4,128)S(1)}, u32[]{:S(2)}, u32[]{:S(2)}) collective-permute-start(f32[1,4,256]{2,1,0:T(4,128)S(1)} %get-tuple-element.44), channel_id=1, source_target_pairs={{0,16},{1,17},{2,18},{3,19},{4,20},{5,21},{6,22},{7,23},{8,24},{9,... | collective-permute-start | bytes 12296 | tf_op jit(solution)/shard_map/ppermute | solution.py:20
  13.2 46.5 %collective-permute-start.7 = (f32[1,4,256]{2,1,0:T(4,128)S(1)}, f32[1,4,256]{2,1,0:T(4,128)S(1)}, u32[]{:S(2)}, u32[]{:S(2)}) collective-permute-start(f32[1,4,256]{2,1,0:T(4,128)S(1)} %get-tuple-element.45), channel_id=1, source_target_pairs={{16,0},{17,1},{18,2},{19,3},{20,4},{21,5},{22,6},{23,7},{24,8},{25... | collective-permute-start | bytes 12296 | tf_op jit(solution)/shard_map/ppermute | solution.py:22
  59.7 4.5 %collective-permute-start.8 = (f32[4,1,256]{2,1,0:T(1,128)S(1)}, f32[4,1,256]{2,1,0:T(1,128)S(1)}, u32[]{:S(2)}, u32[]{:S(2)}) collective-permute-start(f32[4,1,256]{2,1,0:T(1,128)S(1)} %get-tuple-element.42), channel_id=1, source_target_pairs={{0,4},{4,8},{8,12},{1,5},{5,9},{9,13},{2,6},{6,10},{10,14},{3,7},{... | collective-permute-start | bytes 12296 | tf_op jit(solution)/shard_map/ppermute | solution.py:20
  60.9 5.6 %collective-permute-start.9 = (f32[4,1,256]{2,1,0:T(1,128)S(1)}, f32[4,1,256]{2,1,0:T(1,128)S(1)}, u32[]{:S(2)}, u32[]{:S(2)}) collective-permute-start(f32[4,1,256]{2,1,0:T(1,128)S(1)} %get-tuple-element.43), channel_id=1, source_target_pairs={{4,0},{8,4},{12,8},{5,1},{9,5},{13,9},{6,2},{10,6},{14,10},{7,3},{... | collective-permute-start | bytes 12296 | tf_op jit(solution)/shard_map/ppermute | solution.py:22
  66.6 4.8 %collective-permute-start.10 = (f32[4,6,1]{2,1,0:T(8,128)S(1)}, f32[4,6,1]{2,1,0:T(8,128)S(1)}, u32[]{:S(2)}, u32[]{:S(2)}) collective-permute-start(f32[4,6,1]{2,1,0:T(8,128)S(1)} %get-tuple-element.38), channel_id=1, source_target_pairs={{0,1},{1,2},{2,3},{4,5},{5,6},{6,7},{8,9},{9,10},{10,11},{12,13},{... | collective-permute-start | bytes 296 | tf_op jit(solution)/shard_map/ppermute | solution.py:20
  70.0 5.6 %collective-permute-start.11 = (f32[4,6,1]{2,1,0:T(8,128)S(1)}, f32[4,6,1]{2,1,0:T(8,128)S(1)}, u32[]{:S(2)}, u32[]{:S(2)}) collective-permute-start(f32[4,6,1]{2,1,0:T(8,128)S(1)} %get-tuple-element.39), channel_id=1, source_target_pairs={{1,0},{2,1},{3,2},{5,4},{6,5},{7,6},{9,8},{10,9},{11,10},{13,12},{... | collective-permute-start | bytes 296 | tf_op jit(solution)/shard_map/ppermute | solution.py:22
  76.0 4.2 %collective-permute-start.2 = (bf16[16,4,1,256]{3,2,1,0:T(2,128)(2,1)S(1)}, bf16[16,4,1,256]{3,2,1,0:T(2,128)(2,1)S(1)}, u32[]{:S(2)}, u32[]{:S(2)}) collective-permute-start(bf16[16,4,1,256]{3,2,1,0:T(2,128)(2,1)S(1)} %get-tuple-element.24), channel_id=1, source_target_pairs={{0,4},{4,8},{8,12},{1,5},{5,9},{9,13},{2,6},{6,10},{10,14},{3,7},{... | collective-permute-start | bytes 98312 | tf_op jit(solution)/shard_map/ppermute | solution.py:20
  78.8 4.7 %collective-permute-start.3 = (bf16[16,4,1,256]{3,2,1,0:T(2,128)(2,1)S(1)}, bf16[16,4,1,256]{3,2,1,0:T(2,128)(2,1)S(1)}, u32[]{:S(2)}, u32[]{:S(2)}) collective-permute-start(bf16[16,4,1,256]{3,2,1,0:T(2,128)(2,1)S(1)} %get-tuple-element.25), channel_id=1, source_target_pairs={{4,0},{8,4},{12,8},{5,1},{9,5},{13,9},{6,2},{10,6},{14,10},{7,3},{... | collective-permute-start | bytes 98312 | tf_op jit(solution)/shard_map/ppermute | solution.py:22
  83.9 5.8 %collective-permute-start.4 = (bf16[16,4,6,1]{3,2,1,0:T(8,128)(2,1)S(1)}, bf16[16,4,6,1]{3,2,1,0:T(8,128)(2,1)S(1)}, u32[]{:S(2)}, u32[]{:S(2)}) collective-permute-start(bf16[16,4,6,1]{3,2,1,0:T(8,128)(2,1)S(1)} %get-tuple-element.17), channel_id=1, source_target_pairs={{0,1},{1,2},{2,3},{4,5},{5,6},{6,7},{8,9},{9,10},{10,11},{12,13},{... | collective-permute-start | bytes 2312 | tf_op jit(solution)/shard_map/ppermute | solution.py:20
  87.2 6.9 %collective-permute-start.5 = (bf16[16,4,6,1]{3,2,1,0:T(8,128)(2,1)S(1)}, bf16[16,4,6,1]{3,2,1,0:T(8,128)(2,1)S(1)}, u32[]{:S(2)}, u32[]{:S(2)}) collective-permute-start(bf16[16,4,6,1]{3,2,1,0:T(8,128)(2,1)S(1)} %get-tuple-element.16), channel_id=1, source_target_pairs={{1,0},{2,1},{3,2},{5,4},{6,5},{7,6},{9,8},{10,9},{11,10},{13,12},{... | collective-permute-start | bytes 2312 | tf_op jit(solution)/shard_map/ppermute | solution.py:22
  95.5 1.6 copy-start.1
  97.2 0.7 copy-start.2
  97.2 1.2 copy-start.3
  97.8 1.1 copy-start.4
  98.4 1.1 copy-start.5
  98.9 1.1 copy-start.6
  99.5 1.1 copy-start.7
  100.1 1.1 copy-start.8
  101.8 0.9 copy-start
  175.5 5.0 %collective-permute-start.12 = (bf16[16,1,4,256]{3,0,2,1:T(8,128)(2,1)S(1)}, bf16[16,1,4,256]{3,0,2,1:T(8,128)(2,1)S(1)}, u32[]{:S(2)}, u32[]{:S(2)}) collective-permute-start(bf16[16,1,4,256]{3,0,2,1:T(8,128)(2,1)S(1)} %get-tuple-element.26), channel_id=1, source_target_pairs={{0,16},{1,17},{2,18},{3,19},{4,20},{5,21},{6,22},{7,23},{8,24},{9,... | collective-permute-start | bytes 98312 | tf_op jit(solution)/shard_map/ppermute | solution.py:20
  178.9 5.8 %collective-permute-start.13 = (bf16[16,1,4,256]{3,0,2,1:T(8,128)(2,1)S(1)}, bf16[16,1,4,256]{3,0,2,1:T(8,128)(2,1)S(1)}, u32[]{:S(2)}, u32[]{:S(2)}) collective-permute-start(bf16[16,1,4,256]{3,0,2,1:T(8,128)(2,1)S(1)} %get-tuple-element.27), channel_id=1, source_target_pairs={{16,0},{17,1},{18,2},{19,3},{20,4},{21,5},{22,6},{23,7},{24,8},{25... | collective-permute-start | bytes 98312 | tf_op jit(solution)/shard_map/ppermute | solution.py:22
  184.7 2.6 %collective-permute-start.14 = (bf16[16,4,1,256]{3,0,2,1:T(8,128)(2,1)S(1)}, bf16[16,4,1,256]{3,0,2,1:T(8,128)(2,1)S(1)}, u32[]{:S(2)}, u32[]{:S(2)}) collective-permute-start(bf16[16,4,1,256]{3,0,2,1:T(8,128)(2,1)S(1)} %get-tuple-element.22), channel_id=1, source_target_pairs={{0,4},{4,8},{8,12},{1,5},{5,9},{9,13},{2,6},{6,10},{10,14},{3,7},{... | collective-permute-start | bytes 98312 | tf_op jit(solution)/shard_map/ppermute | solution.py:20
  186.0 6.2 %collective-permute-start.15 = (bf16[16,4,1,256]{3,0,2,1:T(8,128)(2,1)S(1)}, bf16[16,4,1,256]{3,0,2,1:T(8,128)(2,1)S(1)}, u32[]{:S(2)}, u32[]{:S(2)}) collective-permute-start(bf16[16,4,1,256]{3,0,2,1:T(8,128)(2,1)S(1)} %get-tuple-element.23), channel_id=1, source_target_pairs={{4,0},{8,4},{12,8},{5,1},{9,5},{13,9},{6,2},{10,6},{14,10},{7,3},{... | collective-permute-start | bytes 98312 | tf_op jit(solution)/shard_map/ppermute | solution.py:22
  192.3 4.1 %collective-permute-start.16 = (bf16[16,4,6,1]{3,0,2,1:T(8,128)(2,1)S(1)}, bf16[16,4,6,1]{3,0,2,1:T(8,128)(2,1)S(1)}, u32[]{:S(2)}, u32[]{:S(2)}) collective-permute-start(bf16[16,4,6,1]{3,0,2,1:T(8,128)(2,1)S(1)} %get-tuple-element.21), channel_id=1, source_target_pairs={{0,1},{1,2},{2,3},{4,5},{5,6},{6,7},{8,9},{9,10},{10,11},{12,13},{... | collective-permute-start | bytes 2312 | tf_op jit(solution)/shard_map/ppermute | solution.py:20
  194.2 6.5 %collective-permute-start.17 = (bf16[16,4,6,1]{3,0,2,1:T(8,128)(2,1)S(1)}, bf16[16,4,6,1]{3,0,2,1:T(8,128)(2,1)S(1)}, u32[]{:S(2)}, u32[]{:S(2)}) collective-permute-start(bf16[16,4,6,1]{3,0,2,1:T(8,128)(2,1)S(1)} %get-tuple-element.20), channel_id=1, source_target_pairs={{1,0},{2,1},{3,2},{5,4},{6,5},{7,6},{9,8},{10,9},{11,10},{13,12},{... | collective-permute-start | bytes 2312 | tf_op jit(solution)/shard_map/ppermute | solution.py:22
